TPU v7x, 32 devices: a whole 2x2x4 slice. The times are simulated.
32 devices in a mesh: replica: 4 (over y, core), fsdp: 8 (over z, x).
Axes of the slice: x: 2, y: 2, z: 4, core: 2. Of those that a mesh axis runs over, the one named last changes fastest.
Arguments:
- layer_input: bfloat16 [2, 4096, 4096], P(None, ('replica', 'fsdp')), may hold values from -6 to 6
- queries: bfloat16 [2, 4096, 4096], P(None, ('replica', 'fsdp')), may hold values from -100 to 100
- keys: bfloat16 [2, 4096, 512], P(None, ('replica', 'fsdp')), may hold values from -8 to 8
- targets: bfloat16 [2, 4096, 4096], P(None, ('replica', 'fsdp')), may hold values from -6 to 6
- value_weight: float32 [4096, 512], P('fsdp'), may hold values from -6 to 6
- outer_momentum: float32 [4096, 512], P('fsdp'), may hold values from -0.6 to 0.6
Outputs:
- new_weight: float32 [4096, 512], P('fsdp')
- new_momentum: float32 [4096, 512], P('fsdp')
All inputs are finite; a program needn't handle non-finite values.
Results may differ from a plain program's by a relative error of at most 0.0017.
Values may be sent and summed in bfloat16 or wider, within the bound.
A program may use at most 64 MiB of HBM per device.

v0:
```python
import functools
import math

import jax
import jax.numpy as jnp
from jax import lax
from jax.experimental import pallas as pl
from jax.experimental.pallas import tpu as pltpu
from jax.sharding import PartitionSpec as P

D = 4096
QH = 32
KVH = 4
HD = 128


beta_one = 0.9
beta_two = 0.95
inner_rate = 0.05
decay_rate = 0.1
outer_rate = 0.7
outer_mu = 0.9


def plain_shards(layer_input, queries, keys, targets, value_weight, outer_momentum):
    inner_steps = layer_input.shape[0]
    length = layer_input.shape[1]
    columns = value_weight.shape[1]
    fsdp_count = lax.axis_size("fsdp")
    replicas = lax.axis_size("replica")
    tok_rep = length * fsdp_count
    group_size = QH // KVH
    adam_floor = math.sqrt(group_size / (tok_rep * D))
    by_features = lax.all_to_all(layer_input, "fsdp", split_axis=2, concat_axis=1, tiled=True)
    causal = jnp.arange(length)[:, None] >= jnp.arange(length)[None, :]
    weights_now = value_weight
    moment_one = jnp.zeros_like(value_weight)
    moment_two = jnp.zeros_like(value_weight)
    for step_index in range(inner_steps):
        inputs = layer_input[step_index]
        shard_bf = weights_now.astype(jnp.bfloat16)
        product = jnp.dot(
            inputs,
            lax.all_gather(shard_bf, "fsdp", axis=0, tiled=True),
            preferred_element_type=jnp.float32,
        )
        values = (product / math.sqrt(D)).astype(jnp.bfloat16)
        query_heads = queries[step_index].reshape(length, KVH, group_size, HD)
        key_heads = keys[step_index].reshape(length, KVH, HD)
        scores = jnp.einsum(
            "qgjd,kgd->gjqk", query_heads, key_heads, preferred_element_type=jnp.float32
        ) / math.sqrt(HD)
        scores = jnp.where(causal, scores, -1e30)
        highest = jnp.max(scores, axis=-1, keepdims=True)
        expd = jnp.exp(scores - highest)
        attention = (expd / jnp.sum(expd, axis=-1, keepdims=True)).astype(jnp.bfloat16)
        attended = jnp.einsum(
            "gjqk,kgd->qgjd",
            attention,
            values.reshape(length, KVH, HD),
            preferred_element_type=jnp.float32,
        ).reshape(length, QH * HD)
        out_grad = ((attended - targets[step_index].astype(jnp.float32)) / tok_rep).astype(
            jnp.bfloat16
        )
        value_grad = (
            jnp.einsum(
                "gjqk,qgjd->kgd",
                attention,
                out_grad.reshape(length, KVH, group_size, HD),
                preferred_element_type=jnp.float32,
            )
            .reshape(length, columns)
            .astype(jnp.bfloat16)
        )
        step_features = by_features[step_index]
        gradient = lax.dot_general(
            step_features,
            lax.all_gather(value_grad, "fsdp", axis=0, tiled=True),
            (((0,), (0,)), ((), ())),
            preferred_element_type=jnp.float32,
        ) / math.sqrt(D)
        moment_one = beta_one * moment_one + (1.0 - beta_one) * gradient
        moment_two = beta_two * moment_two + (1.0 - beta_two) * gradient * gradient
        corrected_one = moment_one / (1.0 - beta_one ** (step_index + 1))
        corrected_two = moment_two / (1.0 - beta_two ** (step_index + 1))
        weights_now = weights_now - inner_rate * (
            corrected_one / (jnp.sqrt(corrected_two) + adam_floor) + decay_rate * weights_now
        )
    total_delta = lax.psum(value_weight - weights_now, "replica")
    mean_delta = total_delta / replicas
    new_momentum = outer_mu * outer_momentum + mean_delta
    new_weight = value_weight - outer_rate * (mean_delta + outer_mu * new_momentum)
    return (new_weight, new_momentum)


MESH = pl.DeviceIdType.MESH


def round_kernel(
    n,
    x_ref,
    q_ref,
    k_ref,
    t_ref,
    w_ref,
    mean_ref,
    feat,
    q_buf,
    k_buf,
    t_buf,
    w_buf,
    mat_hi,
    mat_lo,
    base,
    side_out,
    side_in,
    col_out,
    col_in,
    vgrad,
    grad,
    theta,
    mom_one,
    mom_two,
    wbf,
    acc,
    delta,
    core_in,
    pair_out,
    pair_in,
    total,
    in_s,
    in_r,
    side_s,
    side_r,
    col_s,
    col_r,
    agz_s,
    agz_r,
    agx_s,
    agx_r,
    rep_s,
    rep_r,
    load_s,
):
    steps, length, _ = x_ref.shape
    rows, columns = w_ref.shape
    parts = 2
    width = columns // parts
    wide = [slice(p * width, (p + 1) * width) for p in range(parts)]
    heads = columns // HD
    group = QH // KVH
    tok_rep = length * n
    adam_floor = math.sqrt(group / (tok_rep * D))
    nz = n // 2
    me = lax.axis_index("fsdp")
    rep = lax.axis_index("replica")
    z, px = me // 2, me % 2
    core = rep % 2
    core_peer = rep + 1 - 2 * core
    pair_peer = (rep + 2) % 4
    side = z * 2 + (1 - px)

    def at(dz, dx):
        return ((z + dz + nz) % nz) * 2 + (px + dx) % 2

    def turn(i):
        return (1 - core) * i + core * (nz - i) if i else 0

    order = [*range(1, nz), 0]
    hops = [(i, 1) for i in order] + [(i, 0) for i in range(1, nz)]

    loads = {}

    def load(i, src, dst):
        loads[i] = pltpu.make_async_copy(src, dst, load_s.at[i])
        loads[i].start()

    barrier = pltpu.get_barrier_semaphore()
    for dz, dx in hops:
        pl.semaphore_signal(barrier, inc=1, device_id={"fsdp": at(dz, dx)}, device_id_type=MESH)
    for peer in (core_peer, pair_peer):
        pl.semaphore_signal(barrier, inc=1, device_id={"replica": peer}, device_id_type=MESH)
    load(steps, q_ref, q_buf)
    load(steps + 1, k_ref, k_buf)
    load(steps + 2, t_ref, t_buf)
    load(steps + 3, w_ref, w_buf)
    pl.semaphore_wait(barrier, n + 1)

    def send(src, dst, ssem, rsem, axis, peer):
        copy = pltpu.make_async_remote_copy(
            src_ref=src,
            dst_ref=dst,
            send_sem=ssem,
            recv_sem=rsem,
            device_id={axis: peer},
            device_id_type=MESH,
        )
        copy.start()
        return copy

    def send_inputs(s, only=None):
        copies = {}
        for k, dx in only or hops:
            dz = turn(k)
            peer = at(dz, dx)
            i = dz * 2 + dx
            copies[k, dx] = send(
                x_ref.at[s, :, pl.ds(pl.multiple_of(peer * rows, 128), rows)],
                feat.at[s, me],
                in_s.at[s, i],
                in_r.at[s, i],
                "fsdp",
                peer,
            )
        return copies

    causal = lax.broadcasted_iota(jnp.int32, (length, length), 0) >= lax.broadcasted_iota(
        jnp.int32, (length, length), 1
    )

    def attention_of(s):
        def one(g, carry):
            keys = k_buf[s, :, pl.ds(pl.multiple_of(g * HD, HD), HD)]
            both = jnp.zeros((length, length + HD), jnp.float32)
            for j in range(group):
                cols = pl.ds(pl.multiple_of((g * group + j) * HD, HD), HD)
                scores = lax.dot_general(
                    q_buf[s, :, cols],
                    keys,
                    (((1,), (1,)), ((), ())),
                    preferred_element_type=jnp.float32,
                ) / math.sqrt(HD)
                scores = jnp.where(causal, scores, -1e30)
                highest = jnp.max(scores, axis=-1, keepdims=True)
                expd = jnp.exp(scores - highest)
                att = (expd / jnp.sum(expd, axis=-1, keepdims=True)).astype(jnp.bfloat16)
                both += lax.dot_general(
                    att,
                    jnp.concatenate([att, t_buf[s, :, cols]], axis=1),
                    (((0,), (0,)), ((), ())),
                    preferred_element_type=jnp.float32,
                )
            gram = both[:, :length]
            high = gram.astype(jnp.bfloat16)
            mat_hi[s, g] = high
            mat_lo[s, g] = (gram - high.astype(jnp.float32)).astype(jnp.bfloat16)
            base[s, g] = both[:, length:]
            return carry

        lax.fori_loop(0, heads, one, 0)

    chunk = 32

    def chunks(body):
        def step(i, carry):
            body(pl.ds(pl.multiple_of(i * chunk, chunk), chunk))
            return carry

        lax.fori_loop(0, rows // chunk, step, 0)

    pending = []
    inputs = {0: send_inputs(0)}
    for s in range(steps):
        load(
            s,
            x_ref.at[s, :, pl.ds(pl.multiple_of(me * rows, 128), rows)],
            feat.at[s, me],
        )

    def cast_weights(c):
        wbf[c, :] = w_buf[c, :].astype(jnp.bfloat16)

    loads[steps + 3].wait()
    chunks(cast_weights)
    for i in (*range(steps), steps, steps + 1, steps + 2):
        loads[i].wait()
    for s in range(steps):
        attention_of(s)

    for s in range(steps):
        def partial(j, p):
            return jnp.dot(feat[s, j], wbf[:, wide[p]], preferred_element_type=jnp.float32)

        if s + 1 < steps:
            inputs[s + 1] = send_inputs(s + 1, hops[:2])
        sides = {}
        for k in order:
            inputs[s][k, 1].wait_recv()
            dz = (nz - turn(k)) % nz if k else 0
            for p in range(parts):
                side_out[s, dz, :, wide[p]] = partial(at(dz, 1), p).astype(jnp.bfloat16)
                sides[k, p] = send(
                    side_out.at[s, dz, :, wide[p]],
                    side_in.at[s, dz, :, wide[p]],
                    side_s.at[s, dz, p],
                    side_r.at[s, dz, p],
                    "fsdp",
                    side,
                )
        cols = {}
        for k in order:
            dz = (nz - turn(k)) % nz if k else 0
            if k:
                inputs[s][k, 0].wait_recv()
            for p in range(parts):
                own = partial(at(dz, 0), p)
                sides[k, p].wait_recv()
                own = own + side_in[s, dz, :, wide[p]].astype(jnp.float32)
                if k:
                    col_out[s, dz, :, wide[p]] = own.astype(jnp.bfloat16)
                    cols[k, p] = send(
                        col_out.at[s, dz, :, wide[p]],
                        col_in.at[s, dz, :, wide[p]],
                        col_s.at[s, dz, p],
                        col_r.at[s, dz, p],
                        "fsdp",
                        at(dz, 0),
                    )
                else:
                    acc[:, wide[p]] = own
        pending += [*sides.values(), *cols.values(), *inputs[s].values()]

        def add_block(j, p, first=False):
            term = lax.dot_general(
                feat[s, j],
                vgrad[s, j, :, wide[p]],
                (((0,), (0,)), ((), ())),
                preferred_element_type=jnp.float32,
            )
            if first:
                grad[:, wide[p]] = term
            else:
                grad[:, wide[p]] += term

        def forward(j, i, p):
            block = vgrad.at[s, j, :, wide[p]]
            return send(block, block, agx_s.at[s, i, p], agx_r.at[s, i, p], "fsdp", side)

        zs = {}
        xs = {}
        for p in range(parts):
            summed = acc[:, wide[p]]
            for k in range(1, nz):
                cols[k, p].wait_recv()
            for dz in range(1, nz):
                summed = summed + col_in[s, dz, :, wide[p]].astype(jnp.float32)
            values = (summed / math.sqrt(D)).astype(jnp.bfloat16)
            for i in range(width // HD):
                g = p * (width // HD) + i
                part = values[:, i * HD : (i + 1) * HD]
                vg = jnp.dot(mat_hi[s, g], part, preferred_element_type=jnp.float32)
                vg += jnp.dot(mat_lo[s, g], part, preferred_element_type=jnp.float32)
                vg = (vg - base[s, g]) / tok_rep
                vgrad[s, me, :, g * HD : (g + 1) * HD] = vg.astype(jnp.bfloat16)
            block = vgrad.at[s, me, :, wide[p]]
            for k in range(1, nz):
                dz = turn(k)
                zs[k, p] = send(
                    block, block, agz_s.at[s, dz, p], agz_r.at[s, dz, p], "fsdp", at(dz, 0)
                )
            xs[0, p] = forward(me, 0, p)
        for p in range(parts):
            add_block(me, p, True)
        for p in range(parts):
            for k in range(1, nz):
                zs[k, p].wait_recv()
                xs[k, p] = forward(at(-turn(k), 0), turn(k), p)
                add_block(at(-turn(k), 0), p)
        if s + 1 < steps:
            inputs[s + 1].update(send_inputs(s + 1, hops[2:]))
        for p in range(parts):
            for k in range(nz):
                xs[k, p].wait_recv()
                add_block(at(-turn(k), 1), p)
        pending += [*zs.values(), *xs.values()]

        def adam(c):
            gradient = grad[c, :] / math.sqrt(D)
            one = (1.0 - beta_one) * gradient
            two = (1.0 - beta_two) * gradient * gradient
            if s:
                one = beta_one * mom_one[c, :] + one
                two = beta_two * mom_two[c, :] + two
            now = theta[c, :] if s else w_buf[c, :]
            fixed_one = one / (1.0 - beta_one ** (s + 1))
            fixed_two = two / (1.0 - beta_two ** (s + 1))
            now = now - inner_rate * (
                fixed_one / (jnp.sqrt(fixed_two) + adam_floor) + decay_rate * now
            )
            if s + 1 < steps:
                mom_one[c, :] = one
                mom_two[c, :] = two
                theta[c, :] = now
                wbf[c, :] = now.astype(jnp.bfloat16)
            else:
                delta[c, :] = w_buf[c, :] - now

        if s + 1 < steps:
            chunks(adam)

    half = rows // 2
    piece = half // parts

    def span(which, p):
        return pl.multiple_of(which * half + p * piece, 128)

    def over(start, body):
        def step(i, carry):
            body(pl.ds(pl.multiple_of(start + i * chunk, chunk), chunk))
            return carry

        lax.fori_loop(0, piece // chunk, step, 0)

    first, second, third = [], [], []
    for p in range(parts):
        over(span(1 - core, p), adam)
        first.append(
            send(
                delta.at[pl.ds(span(1 - core, p), piece)],
                core_in.at[pl.ds(p * piece, piece)],
                rep_s.at[0, p],
                rep_r.at[0, p],
                "replica",
                core_peer,
            )
        )
    for p in range(parts):
        over(span(core, p), adam)
        first[p].wait_recv()
        rows_p = pl.ds(p * piece, piece)
        pair_out[rows_p, :] = (
            delta[pl.ds(span(core, p), piece), :] + core_in[rows_p, :]
        ).astype(jnp.bfloat16)
        second.append(
            send(
                pair_out.at[rows_p],
                pair_in.at[rows_p],
                rep_s.at[1, p],
                rep_r.at[1, p],
                "replica",
                pair_peer,
            )
        )

    def finish(c):
        mean_ref[c, :] = total[c, :] / 4

    for p in range(parts):
        second[p].wait_recv()
        rows_p = pl.ds(p * piece, piece)
        mine = pl.ds(span(core, p), piece)
        total[mine, :] = pair_out[rows_p, :].astype(jnp.float32) + pair_in[
            rows_p, :
        ].astype(jnp.float32)
        third.append(
            send(
                total.at[mine],
                total.at[mine],
                rep_s.at[2, p],
                rep_r.at[2, p],
                "replica",
                core_peer,
            )
        )
        over(span(core, p), finish)
    for p in range(parts):
        third[p].wait_recv()
        over(span(1 - core, p), finish)
    for copy in pending + first + second + third:
        copy.wait_send()


def shards(layer_input, queries, keys, targets, value_weight, outer_momentum):
    n = lax.axis_size("fsdp")
    replicas = lax.axis_size("replica")
    rows, columns = value_weight.shape
    steps, length, _ = layer_input.shape
    if rows % 512 or columns % (2 * HD) or n % 2 or replicas != 4 or length % 128:
        return plain_shards(layer_input, queries, keys, targets, value_weight, outer_momentum)
    nz = n // 2
    heads = columns // HD
    bf, f32 = jnp.bfloat16, jnp.float32
    dma = pltpu.SemaphoreType.DMA
    out = jax.ShapeDtypeStruct((rows, columns), f32)
    mean_delta = pl.pallas_call(
        functools.partial(round_kernel, n),
        out_shape=out,
        in_specs=[pl.BlockSpec(memory_space=pl.ANY)] * 5,
        out_specs=pl.BlockSpec(memory_space=pltpu.VMEM),
        scratch_shapes=[
            pltpu.VMEM((steps, n, length, rows), bf),
            pltpu.VMEM(queries.shape, bf),
            pltpu.VMEM(keys.shape, bf),
            pltpu.VMEM(targets.shape, bf),
            pltpu.VMEM((rows, columns), f32),
            pltpu.VMEM((steps, heads, length, length), bf),
            pltpu.VMEM((steps, heads, length, length), bf),
            pltpu.VMEM((steps, heads, length, HD), f32),
            pltpu.VMEM((steps, nz, length, columns), bf),
            pltpu.VMEM((steps, nz, length, columns), bf),
            pltpu.VMEM((steps, nz, length, columns), bf),
            pltpu.VMEM((steps, nz, length, columns), bf),
            pltpu.VMEM((steps, n, length, columns), bf),
            pltpu.VMEM((rows, columns), f32),
            pltpu.VMEM((rows, columns), f32),
            pltpu.VMEM((rows, columns), f32),
            pltpu.VMEM((rows, columns), f32),
            pltpu.VMEM((rows, columns), bf),
            pltpu.VMEM((length, columns), f32),
            pltpu.VMEM((rows, columns), f32),
            pltpu.VMEM((rows // 2, columns), f32),
            pltpu.VMEM((rows // 2, columns), bf),
            pltpu.VMEM((rows // 2, columns), bf),
            pltpu.VMEM((rows, columns), f32),
            dma((steps, n)),
            dma((steps, n)),
            dma((steps, nz, 2)),
            dma((steps, nz, 2)),
            dma((steps, nz, 2)),
            dma((steps, nz, 2)),
            dma((steps, nz, 2)),
            dma((steps, nz, 2)),
            dma((steps, nz, 2)),
            dma((steps, nz, 2)),
            dma((3, 2)),
            dma((3, 2)),
            dma((steps + 4,)),
        ],
        compiler_params=pltpu.CompilerParams(collective_id=0, has_side_effects=True),
    )(layer_input, queries, keys, targets, value_weight)
    new_momentum = outer_mu * outer_momentum + mean_delta
    new_weight = value_weight - outer_rate * (mean_delta + outer_mu * new_momentum)
    return (new_weight, new_momentum)


def solution(mesh):
    in_specs = (
        P(None, ("replica", "fsdp"), None),
        P(None, ("replica", "fsdp"), None),
        P(None, ("replica", "fsdp"), None),
        P(None, ("replica", "fsdp"), None),
        P("fsdp", None),
        P("fsdp", None),
    )
    out_specs = (P("fsdp", None), P("fsdp", None))
    return jax.shard_map(shards, mesh=mesh, in_specs=in_specs, out_specs=out_specs, check_vma=False)
```

profile of v0, /device:TPU:0, one launch (start us, length us, event | category | flops | bytes accessed | tf_op | source)
XLA Modules:
  0.0 119.7 jit_solution(16036313221647872617)
XLA Ops:
  0.6 0.0 copy-start
  0.6 0.0 copy-start.1
  0.7 116.0 %shard_map.77 = f32[512,512]{1,0:T(8,128)} custom-call(bf16[2,128,4096]{2,1,0:T(8,128)(2,1)} %x_ref.1, bf16[2,128,4096]{2,1,0:T(8,128)(2,1)} %q_ref.1, bf16[2,128,512]{2,1,0:T(8,128)(2,1)} %k_ref.1, bf16[2,128,4096]{2,1,0:T(8,128)(2,1)} %t_ref.1, f32[512,512]{1,0:T(8,128)} %w_ref.1), custom_call_target="tpu_custom_call" | custom-call | tf_op jit(solution)/shard_map/pallas_call | solution.py:486
  116.7 0.0 copy-done
  116.7 0.0 copy-done.1
  116.7 2.9 %multiply_subtract_fusion = (f32[512,512]{1,0:T(8,128)}, f32[512,512]{1,0:T(8,128)}) fusion(f32[512,512]{1,0:T(8,128)S(1)} %copy-done, f32[512,512]{1,0:T(8,128)} %shard_map.77, f32[512,512]{1,0:T(8,128)S(1)} %copy-done.1), kind=kLoop, calls=%fused_computation | loop fusion | flops 1572864 | bytes 5242880 | tf_op jit(solution)/shard_map/sub | solution.py:533
Async XLA Ops:
  0.6 116.1 %copy-start = (f32[512,512]{1,0:T(8,128)S(1)}, f32[512,512]{1,0:T(8,128)}, u32[]{:S(2)}) copy-start(f32[512,512]{1,0:T(8,128)} %w_ref.1) | copy-start | bytes 3145732
  0.6 116.1 %copy-start.1 = (f32[512,512]{1,0:T(8,128)S(1)}, f32[512,512]{1,0:T(8,128)}, u32[]{:S(2)}) copy-start(f32[512,512]{1,0:T(8,128)} %param.11) | copy-start | bytes 3145732
where the time goes:
time: 120 us
  Pallas kernels  116 us (97%)
  other arithmetic  2.93 us (2%)
    pallas_call x1, Pallas kernels, shards(): pl.pallas_call(functools.partial(round_kernel, n), out_shape=out, in_spec...  116 us
    sub x1, other arithmetic, shards(): value_weight - outer_rate * (mean_delta + outer_mu * new_momentum)  2.93 us

commit v1 on v0

v1 whole, which is shorter than its diff:
```python
import math

import jax
import jax.numpy as jnp
from jax import lax
from jax.experimental import pallas as pl
from jax.experimental.pallas import tpu as pltpu
from jax.sharding import PartitionSpec as P

D = 4096
QH = 32
KVH = 4
HD = 128


beta_one = 0.9
beta_two = 0.95
inner_rate = 0.05
decay_rate = 0.1
outer_rate = 0.7
outer_mu = 0.9


def plain_shards(layer_input, queries, keys, targets, value_weight, outer_momentum):
    inner_steps = layer_input.shape[0]
    length = layer_input.shape[1]
    columns = value_weight.shape[1]
    fsdp_count = lax.axis_size("fsdp")
    replicas = lax.axis_size("replica")
    tok_rep = length * fsdp_count
    group_size = QH // KVH
    adam_floor = math.sqrt(group_size / (tok_rep * D))
    by_features = lax.all_to_all(layer_input, "fsdp", split_axis=2, concat_axis=1, tiled=True)
    causal = jnp.arange(length)[:, None] >= jnp.arange(length)[None, :]
    weights_now = value_weight
    moment_one = jnp.zeros_like(value_weight)
    moment_two = jnp.zeros_like(value_weight)
    for step_index in range(inner_steps):
        inputs = layer_input[step_index]
        shard_bf = weights_now.astype(jnp.bfloat16)
        product = jnp.dot(
            inputs,
            lax.all_gather(shard_bf, "fsdp", axis=0, tiled=True),
            preferred_element_type=jnp.float32,
        )
        values = (product / math.sqrt(D)).astype(jnp.bfloat16)
        query_heads = queries[step_index].reshape(length, KVH, group_size, HD)
        key_heads = keys[step_index].reshape(length, KVH, HD)
        scores = jnp.einsum(
            "qgjd,kgd->gjqk", query_heads, key_heads, preferred_element_type=jnp.float32
        ) / math.sqrt(HD)
        scores = jnp.where(causal, scores, -1e30)
        highest = jnp.max(scores, axis=-1, keepdims=True)
        expd = jnp.exp(scores - highest)
        attention = (expd / jnp.sum(expd, axis=-1, keepdims=True)).astype(jnp.bfloat16)
        attended = jnp.einsum(
            "gjqk,kgd->qgjd",
            attention,
            values.reshape(length, KVH, HD),
            preferred_element_type=jnp.float32,
        ).reshape(length, QH * HD)
        out_grad = ((attended - targets[step_index].astype(jnp.float32)) / tok_rep).astype(
            jnp.bfloat16
        )
        value_grad = (
            jnp.einsum(
                "gjqk,qgjd->kgd",
                attention,
                out_grad.reshape(length, KVH, group_size, HD),
                preferred_element_type=jnp.float32,
            )
            .reshape(length, columns)
            .astype(jnp.bfloat16)
        )
        step_features = by_features[step_index]
        gradient = lax.dot_general(
            step_features,
            lax.all_gather(value_grad, "fsdp", axis=0, tiled=True),
            (((0,), (0,)), ((), ())),
            preferred_element_type=jnp.float32,
        ) / math.sqrt(D)
        moment_one = beta_one * moment_one + (1.0 - beta_one) * gradient
        moment_two = beta_two * moment_two + (1.0 - beta_two) * gradient * gradient
        corrected_one = moment_one / (1.0 - beta_one ** (step_index + 1))
        corrected_two = moment_two / (1.0 - beta_two ** (step_index + 1))
        weights_now = weights_now - inner_rate * (
            corrected_one / (jnp.sqrt(corrected_two) + adam_floor) + decay_rate * weights_now
        )
    total_delta = lax.psum(value_weight - weights_now, "replica")
    mean_delta = total_delta / replicas
    new_momentum = outer_mu * outer_momentum + mean_delta
    new_weight = value_weight - outer_rate * (mean_delta + outer_mu * new_momentum)
    return (new_weight, new_momentum)


MESH = pl.DeviceIdType.MESH


def round_kernel(
    x_ref,
    q_ref,
    k_ref,
    t_ref,
    w_ref,
    mean_ref,
    feat,
    q_buf,
    k_buf,
    t_buf,
    w_buf,
    wb,
    w_now,
    mat,
    base,
    pair_out,
    pair_in,
    red_out,
    red_in,
    vgrad,
    grad,
    first_update,
    sy_out,
    sy_in,
    s_own,
    halves,
    tot_mine,
    tot_other,
    in_s,
    in_r,
    w_s,
    w_r,
    mat_s,
    mat_r,
    pair_s,
    pair_r,
    red_s,
    red_r,
    ag_s,
    ag_r,
    fw_s,
    fw_r,
    fin_s,
    fin_r,
    load_s,
):
    steps, length, _ = x_ref.shape
    rows, columns = w_ref.shape
    parts = 2
    width = columns // parts
    wide = [slice(p * width, (p + 1) * width) for p in range(parts)]
    heads = columns // HD
    group = QH // KVH
    quad = 4 * length
    tok_rep = 2 * quad
    adam_floor = math.sqrt(group / (tok_rep * D))
    shrink = 1.0 - inner_rate * decay_rate
    me = lax.axis_index("fsdp")
    rep = lax.axis_index("replica")
    x = me % 2
    low = (me // 2) % 2
    half = me // 4
    y = rep // 2
    core = rep % 2
    sel = (half + core) % 2
    far = sel == 1
    near = sel == 0

    def device(h, l, xx, yy, cc):
        return {"replica": yy * 2 + cc, "fsdp": (h * 2 + l) * 2 + xx}

    core_peer = device(half, low, x, y, 1 - core)
    y_peer = device(half, low, x, 1 - y, core)
    partner = device(core, low, x, y, half)

    def mate(a, b):
        return device(half, (low + a) % 2, (x + b) % 2, y, core)

    def offset(a, b):
        return (((low + a) % 2) * 2 + (x + b) % 2) * length

    quads = [(1, 1), (0, 1), (1, 0), (0, 0)]
    mine = pl.multiple_of(core * quad, quad)
    theirs = pl.multiple_of((1 - core) * quad, quad)

    def at(start, size):
        return pl.ds(pl.multiple_of(start, 32), size)

    loads = {}

    def load(i, src, dst):
        loads[i] = pltpu.make_async_copy(src, dst, load_s.at[i])
        loads[i].start()

    barrier = pltpu.get_barrier_semaphore()
    count = 0
    for dh in range(2):
        for dl in range(2):
            for dx in range(2):
                for dc in range(2):
                    if dh + dl + dx + dc:
                        peer = device(
                            (half + dh) % 2, (low + dl) % 2, (x + dx) % 2, y, (core + dc) % 2
                        )
                        pl.semaphore_signal(barrier, inc=1, device_id=peer, device_id_type=MESH)
                        count += 1
    pl.semaphore_signal(barrier, inc=1, device_id=y_peer, device_id_type=MESH)
    load(0, w_ref, w_buf)
    load(1, q_ref, q_buf)
    load(2, k_ref, k_buf)
    load(3, t_ref, t_buf)
    pl.semaphore_wait(barrier, count + 1)

    pending, far_pending, near_pending = [], [], []

    def remote(src, dst, ssem, rsem, peer):
        return pltpu.make_async_remote_copy(
            src_ref=src,
            dst_ref=dst,
            send_sem=ssem,
            recv_sem=rsem,
            device_id=peer,
            device_id_type=MESH,
        )

    def send(*args):
        copy = remote(*args)
        copy.start()
        pending.append(copy)
        return copy

    def send_if(cond, keep, *args):
        copy = remote(*args)

        @pl.when(cond)
        def _():
            copy.start()

        keep.append(copy)
        return copy

    def wait_if(cond, copy):
        @pl.when(cond)
        def _():
            copy.wait_recv()

    def send_inputs(s, picks):
        for a, b, dc in picks:
            l2, x2, c2 = (low + a) % 2, (x + b) % 2, (core + dc) % 2
            i = a * 4 + b * 2 + dc
            src = x_ref.at[
                s, :, pl.ds(pl.multiple_of(((c2 * 2 + l2) * 2 + x2) * rows, 128), rows)
            ]
            dst = feat.at[s, at(me * length, length)]
            args = (src, dst, in_s.at[s, i], in_r.at[s, me], device(core, l2, x2, y, c2))
            if i:
                send(*args)
            else:
                send_if(far, far_pending, *args)

                @pl.when(near)
                def _():
                    pltpu.make_async_copy(src, dst, in_r.at[s, me]).start()

    def wait_input(s, j):
        slot = feat.at[s, at(j * length, length)]
        remote(slot, slot, in_s.at[s, 0], in_r.at[s, j], core_peer).wait_recv()

    causal = lax.broadcasted_iota(jnp.int32, (length, length), 0) >= lax.broadcasted_iota(
        jnp.int32, (length, length), 1
    )

    def attention_of(s):
        def one(g, carry):
            keys = k_buf[s, :, pl.ds(pl.multiple_of(g * HD, HD), HD)]
            both = jnp.zeros((length, length + HD), jnp.float32)
            for j in range(group):
                cols = pl.ds(pl.multiple_of((g * group + j) * HD, HD), HD)
                scores = lax.dot_general(
                    q_buf[s, :, cols],
                    keys,
                    (((1,), (1,)), ((), ())),
                    preferred_element_type=jnp.float32,
                ) / math.sqrt(HD)
                scores = jnp.where(causal, scores, -1e30)
                highest = jnp.max(scores, axis=-1, keepdims=True)
                expd = jnp.exp(scores - highest)
                att = (expd / jnp.sum(expd, axis=-1, keepdims=True)).astype(jnp.bfloat16)
                both += lax.dot_general(
                    att,
                    jnp.concatenate([att, t_buf[s, :, cols]], axis=1),
                    (((0,), (0,)), ((), ())),
                    preferred_element_type=jnp.float32,
                )
            mat[0, s, g] = both[:, :length].astype(jnp.bfloat16)
            base[0, s, g] = both[:, length:].astype(jnp.bfloat16)
            return carry

        lax.fori_loop(0, heads, one, 0)
        first = send_if(
            far, far_pending, mat.at[0, s], mat.at[1, s], mat_s.at[s, 0], mat_r.at[s, 0], partner
        )
        second = send_if(
            far, far_pending, base.at[0, s], base.at[1, s], mat_s.at[s, 1], mat_r.at[s, 1], partner
        )
        return first, second

    chunk = 32

    def over(start, size, body):
        def step(i, carry):
            body(i * chunk)
            return carry

        lax.fori_loop(0, size // chunk, step, 0)

    order = [(a, b, dc) for a, b in quads for dc in (1, 0)]
    send_inputs(0, order[:4])
    loads[0].wait()

    def cast_weights(r):
        wb[0, at(r, chunk), :] = w_buf[at(r, chunk), :].astype(jnp.bfloat16)

    over(0, rows, cast_weights)
    mid = rows // 2
    w_mine = at(y * mid, mid)
    w_cross = send_if(
        far, far_pending, wb.at[0, w_mine], wb.at[1, w_mine], w_s.at[0], w_r.at[0], partner
    )
    send_inputs(0, order[4:])
    for i in (1, 2, 3):
        loads[i].wait()
    mats = [attention_of(0)]
    wait_if(far, w_cross)
    w_relay = send_if(
        far, far_pending, wb.at[1, w_mine], wb.at[1, w_mine], w_s.at[1], w_r.at[1], y_peer
    )
    later = {s: list(order) for s in range(1, steps)}
    for s in range(1, steps):
        send_inputs(s, later[s][:2])
        later[s] = later[s][2:]
        mats.append(attention_of(s))
    wait_if(far, w_relay)

    def weights(s, p):
        return wb[sel, :, wide[p]] if s == 0 else w_now[:, wide[p]]

    for s in range(steps):
        def feed(k):
            if s + 1 < steps:
                send_inputs(s + 1, later[s + 1][:k])
                later[s + 1] = later[s + 1][k:]

        for a, b in quads:
            wait_input(s, (1 - core) * 4 + ((low + a) % 2) * 2 + (x + b) % 2)
        pairs = {}
        for a in (1, 0):
            start = ((low + a) % 2) * 2 * length
            span = at(start, 2 * length)
            for p in range(parts):
                part = jnp.dot(
                    feat[s, at(theirs + start, 2 * length)],
                    weights(s, p),
                    preferred_element_type=jnp.float32,
                )
                pair_out[s, span, wide[p]] = part.astype(jnp.bfloat16)
                pairs[a, p] = send(
                    pair_out.at[s, span, wide[p]],
                    pair_in.at[s, span, wide[p]],
                    pair_s.at[s, a, p],
                    pair_r.at[s, a, p],
                    core_peer,
                )
        for a, b in quads:
            wait_input(s, core * 4 + ((low + a) % 2) * 2 + (x + b) % 2)
        reds = {}
        for p in range(parts):
            for a in (1, 0):
                start = ((low + a) % 2) * 2 * length
                span = at(start, 2 * length)
                own = jnp.dot(
                    feat[s, at(mine + start, 2 * length)],
                    weights(s, p),
                    preferred_element_type=jnp.float32,
                )
                pairs[a, p].wait_recv()
                own = own + pair_in[s, span, wide[p]].astype(jnp.float32)
                red_out[s, span, wide[p]] = own.astype(jnp.bfloat16)
                for b in (1, 0):
                    if a + b:
                        reds[a, b, p] = send(
                            red_out.at[s, at(offset(a, b), length), wide[p]],
                            red_in.at[s, a * 2 + b, :, wide[p]],
                            red_s.at[s, a * 2 + b, p],
                            red_r.at[s, a * 2 + b, p],
                            mate(a, b),
                        )
        feed(2)
        for copy in mats[s]:
            wait_if(far, copy)
        gathers, passes = {}, {}
        slot = at(me_slot(core, low, x) * length, length)
        for p in range(parts):
            summed = red_out[s, at(offset(0, 0), length), wide[p]].astype(jnp.float32)
            for a, b in quads[:3]:
                reds[a, b, p].wait_recv()
                summed = summed + red_in[s, a * 2 + b, :, wide[p]].astype(jnp.float32)
            values = (summed / math.sqrt(D)).astype(jnp.bfloat16)
            for i in range(width // HD):
                g = p * (width // HD) + i
                part = values[:, i * HD : (i + 1) * HD]
                vg = jnp.dot(mat[sel, s, g], part, preferred_element_type=jnp.float32)
                vg = (vg - base[sel, s, g].astype(jnp.float32)) / tok_rep
                vgrad[s, slot, g * HD : (g + 1) * HD] = vg.astype(jnp.bfloat16)
            block = vgrad.at[s, slot, wide[p]]
            for a, b in quads[:3]:
                i = a * 2 + b
                gathers[a, b, p] = send(
                    block, block, ag_s.at[s, i, p], ag_r.at[s, i, p], mate(a, b)
                )
            passes[0, 0, p] = send(
                block, block, fw_s.at[s, 0, p], fw_r.at[s, 0, p], core_peer
            )
        feed(2)

        def add_quad(start, p, first):
            term = lax.dot_general(
                feat[s, at(start, quad)],
                vgrad[s, at(start, quad), wide[p]],
                (((0,), (0,)), ((), ())),
                preferred_element_type=jnp.float32,
            )
            if first:
                grad[s, :, wide[p]] = term
            else:
                grad[s, :, wide[p]] += term

        for p in range(parts):
            for a, b in quads[2::-1]:
                gathers[a, b, p].wait_recv()
                i = a * 2 + b
                block = vgrad.at[s, at(mine + offset(a, b), length), wide[p]]
                passes[a, b, p] = send(
                    block, block, fw_s.at[s, i, p], fw_r.at[s, i, p], core_peer
                )
            add_quad(mine, p, True)
        feed(8)
        for p in range(parts):
            for a, b in quads:
                passes[a, b, p].wait_recv()
            add_quad(theirs, p, False)

        def adam(r, keep):
            c = at(r, chunk)
            one, two = 0.0, 0.0
            for i in range(s + 1):
                gradient = grad[i, c, :] / math.sqrt(D)
                one = beta_one * one + (1.0 - beta_one) * gradient
                two = beta_two * two + (1.0 - beta_two) * gradient * gradient
            fixed_one = one / (1.0 - beta_one ** (s + 1))
            fixed_two = two / (1.0 - beta_two ** (s + 1))
            update = fixed_one / (jnp.sqrt(fixed_two) + adam_floor)
            keep(c, update)

        if s + 1 < steps:

            def keep(c, update):
                before = wb[sel, c, :].astype(jnp.float32)
                first_update[c, :] = update
                w_now[c, :] = (before * shrink - inner_rate * update).astype(jnp.bfloat16)

            over(0, rows, lambda r: adam(r, keep))

    def moved(c, update):
        return inner_rate * (shrink * first_update[c, :] + update)

    pieces = 2
    size = mid // pieces
    sub = size // 2
    firsts, seconds, thirds, fourths, fifths = [], [], [], [], []
    for p in range(pieces):

        def out_piece(r):
            def put(c, update):
                sy_out[at(p * size + r, chunk), :] = moved(c, update).astype(jnp.bfloat16)

            adam((1 - y) * mid + p * size + r, put)

        over(0, size, out_piece)
        piece = at(p * size, size)
        firsts.append(
            send(sy_out.at[piece], sy_in.at[piece], fin_s.at[0, p], fin_r.at[0, p], y_peer)
        )
    for p in range(pieces):

        def own_piece(r):
            def put(c, update):
                s_own[at(p * size + r, chunk), :] = moved(c, update)

            adam(y * mid + p * size + r, put)

        over(0, size, own_piece)
    for p in range(pieces):
        piece = at(p * size, size)
        firsts[p].wait_recv()

        def join(r):
            c = at(p * size + r, chunk)
            halves[2 * sel, c, :] = (s_own[c, :] + sy_in[c, :].astype(jnp.float32)).astype(
                jnp.bfloat16
            )

        over(0, size, join)
        seconds.append(
            send_if(
                near,
                near_pending,
                halves.at[0, piece],
                halves.at[0, piece],
                fin_s.at[1, p],
                fin_r.at[1, p],
                core_peer,
            )
        )
        thirds.append(
            send_if(
                far,
                far_pending,
                halves.at[2, piece],
                halves.at[1, piece],
                fin_s.at[2, p],
                fin_r.at[2, p],
                partner,
            )
        )
    replicas = 4
    for p in range(pieces):
        piece = at(p * size, size)
        wait_if(far, thirds[p])
        fourths.append(
            send_if(
                far,
                far_pending,
                halves.at[1, piece],
                halves.at[1, piece],
                fin_s.at[3, p],
                fin_r.at[3, p],
                core_peer,
            )
        )
        wait_if(far, seconds[p])
        wait_if(near, fourths[p])

        def total(r):
            c = at(p * size + r, chunk)
            both = (
                halves[0, c, :].astype(jnp.float32) + halves[1, c, :].astype(jnp.float32)
            ).astype(jnp.bfloat16)
            tot_mine[c, :] = both
            mean_ref[at(y * mid + p * size + r, chunk), :] = both.astype(jnp.float32) / replicas

        over(0, size, total)
        bit = at(p * size + core * sub, sub)
        fifths.append(
            send(tot_mine.at[bit], tot_other.at[bit], fin_s.at[4, p], fin_r.at[4, p], y_peer)
        )
    sixths = []
    for p in range(pieces):
        bit = at(p * size + core * sub, sub)
        fifths[p].wait_recv()
        sixths.append(
            send(tot_other.at[bit], tot_other.at[bit], fin_s.at[5, p], fin_r.at[5, p], core_peer)
        )
    for p in range(pieces):
        sixths[p].wait_recv()

        def finish(r):
            c = at(p * size + r, chunk)
            mean_ref[at((1 - y) * mid + p * size + r, chunk), :] = (
                tot_other[c, :].astype(jnp.float32) / replicas
            )

        over(0, size, finish)
    for copy in pending:
        copy.wait_send()

    @pl.when(far)
    def _():
        for copy in far_pending:
            copy.wait_send()

    @pl.when(near)
    def _():
        for copy in near_pending:
            copy.wait_send()


def me_slot(core, low, x):
    return (core * 2 + low) * 2 + x


def shards(layer_input, queries, keys, targets, value_weight, outer_momentum):
    n = lax.axis_size("fsdp")
    replicas = lax.axis_size("replica")
    rows, columns = value_weight.shape
    steps, length, _ = layer_input.shape
    if rows % 512 or columns % (2 * HD) or n != 8 or replicas != 4 or length % 128 or steps != 2:
        return plain_shards(layer_input, queries, keys, targets, value_weight, outer_momentum)
    heads = columns // HD
    bf, f32 = jnp.bfloat16, jnp.float32
    dma = pltpu.SemaphoreType.DMA
    out = jax.ShapeDtypeStruct((rows, columns), f32)
    mean_update = pl.pallas_call(
        round_kernel,
        out_shape=out,
        in_specs=[pl.BlockSpec(memory_space=pl.ANY)] * 5,
        out_specs=pl.BlockSpec(memory_space=pltpu.VMEM),
        scratch_shapes=[
            pltpu.VMEM((steps, n * length, rows), bf),
            pltpu.VMEM(queries.shape, bf),
            pltpu.VMEM(keys.shape, bf),
            pltpu.VMEM(targets.shape, bf),
            pltpu.VMEM((rows, columns), f32),
            pltpu.VMEM((2, rows, columns), bf),
            pltpu.VMEM((rows, columns), bf),
            pltpu.VMEM((2, steps, heads, length, length), bf),
            pltpu.VMEM((2, steps, heads, length, HD), bf),
            pltpu.VMEM((steps, 4 * length, columns), bf),
            pltpu.VMEM((steps, 4 * length, columns), bf),
            pltpu.VMEM((steps, 4 * length, columns), bf),
            pltpu.VMEM((steps, 4, length, columns), bf),
            pltpu.VMEM((steps, n * length, columns), bf),
            pltpu.VMEM((steps, rows, columns), f32),
            pltpu.VMEM((rows, columns), f32),
            pltpu.VMEM((rows // 2, columns), bf),
            pltpu.VMEM((rows // 2, columns), bf),
            pltpu.VMEM((rows // 2, columns), f32),
            pltpu.VMEM((3, rows // 2, columns), bf),
            pltpu.VMEM((rows // 2, columns), bf),
            pltpu.VMEM((rows // 2, columns), bf),
            dma((steps, n)),
            dma((steps, n)),
            dma((2,)),
            dma((2,)),
            dma((steps, 2)),
            dma((steps, 2)),
            dma((steps, 2, 2)),
            dma((steps, 2, 2)),
            dma((steps, 4, 2)),
            dma((steps, 4, 2)),
            dma((steps, 4, 2)),
            dma((steps, 4, 2)),
            dma((steps, 4, 2)),
            dma((steps, 4, 2)),
            dma((6, 2)),
            dma((6, 2)),
            dma((4,)),
        ],
        compiler_params=pltpu.CompilerParams(collective_id=0, has_side_effects=True),
    )(layer_input, queries, keys, targets, value_weight)
    kept = (1.0 - inner_rate * decay_rate) ** steps
    mean_delta = (1.0 - kept) * value_weight + mean_update
    new_momentum = outer_mu * outer_momentum + mean_delta
    new_weight = value_weight - outer_rate * (mean_delta + outer_mu * new_momentum)
    return (new_weight, new_momentum)


def solution(mesh):
    in_specs = (
        P(None, ("replica", "fsdp"), None),
        P(None, ("replica", "fsdp"), None),
        P(None, ("replica", "fsdp"), None),
        P(None, ("replica", "fsdp"), None),
        P("fsdp", None),
        P("fsdp", None),
    )
    out_specs = (P("fsdp", None), P("fsdp", None))
    return jax.shard_map(shards, mesh=mesh, in_specs=in_specs, out_specs=out_specs, check_vma=False)
```

time: 120 us -> 117 us (0.975)
  Pallas kernels: 116 us -> 113 us
    pallas_call x1, Pallas kernels: 116 us -> 113 us  [shards(): pl.pallas_call(round_kernel, out_shape=out, in_specs=[pl.BlockSpec(memory...]
where the time goes in v1:
time: 117 us; the launch traced here: 116 us
  Pallas kernels  113 us (97%)
  other arithmetic  2.93 us (3%)
    pallas_call x1, Pallas kernels, shards(): pl.pallas_call(round_kernel, out_shape=out, in_specs=[pl.BlockSpec(memory...  113 us
    sub x1, other arithmetic, shards(): value_weight - outer_rate * (mean_delta + outer_mu * new_momentum)  2.93 us

profile of v1, /device:TPU:0, one launch (start us, length us, event | category | flops | bytes accessed | tf_op | source)
XLA Modules:
  0.0 116.4 jit_solution(3637499475415229872)
XLA Ops:
  0.6 0.0 copy-start
  0.6 0.0 copy-start.1
  0.7 112.8 %shard_map.77 = f32[512,512]{1,0:T(8,128)} custom-call(bf16[2,128,4096]{2,1,0:T(8,128)(2,1)} %x_ref.1, bf16[2,128,4096]{2,1,0:T(8,128)(2,1)} %q_ref.1, bf16[2,128,512]{2,1,0:T(8,128)(2,1)} %k_ref.1, bf16[2,128,4096]{2,1,0:T(8,128)(2,1)} %t_ref.1, f32[512,512]{1,0:T(8,128)} %w_ref.1), custom_call_target="tpu_custom_call" | custom-call | tf_op jit(solution)/shard_map/pallas_call | solution.py:612
  113.5 0.0 copy-done
  113.5 0.0 copy-done.1
  113.5 2.9 %multiply_subtract_fusion = (f32[512,512]{1,0:T(8,128)}, f32[512,512]{1,0:T(8,128)}) fusion(f32[512,512]{1,0:T(8,128)S(1)} %copy-done, f32[512,512]{1,0:T(8,128)} %shard_map.77, f32[512,512]{1,0:T(8,128)S(1)} %copy-done.1), kind=kLoop, calls=%fused_computation | loop fusion | flops 2097152 | bytes 5242880 | tf_op jit(solution)/shard_map/sub | solution.py:663
Async XLA Ops:
  0.6 112.9 %copy-start = (f32[512,512]{1,0:T(8,128)S(1)}, f32[512,512]{1,0:T(8,128)}, u32[]{:S(2)}) copy-start(f32[512,512]{1,0:T(8,128)} %w_ref.1) | copy-start | bytes 3145732
  0.6 112.9 %copy-start.1 = (f32[512,512]{1,0:T(8,128)S(1)}, f32[512,512]{1,0:T(8,128)}, u32[]{:S(2)}) copy-start(f32[512,512]{1,0:T(8,128)} %param.11) | copy-start | bytes 3145732

commit v2 on v1

--- a/solution.py
+++ b/solution.py
@@ -110,6 +110,7 @@
     w_buf,
     wb,
     w_now,
+    own_part,
     mat,
     base,
     pair_out,
@@ -164,6 +165,8 @@
     sel = (half + core) % 2
     far = sel == 1
     near = sel == 0
+    beside = jnp.logical_and(far, low != half)
+    outer = jnp.logical_and(far, low == half)
 
     def device(h, l, xx, yy, cc):
         return {"replica": yy * 2 + cc, "fsdp": (h * 2 + l) * 2 + xx}
@@ -179,8 +182,6 @@
         return (((low + a) % 2) * 2 + (x + b) % 2) * length
 
     quads = [(1, 1), (0, 1), (1, 0), (0, 0)]
-    mine = pl.multiple_of(core * quad, quad)
-    theirs = pl.multiple_of((1 - core) * quad, quad)
 
     def at(start, size):
         return pl.ds(pl.multiple_of(start, 32), size)
@@ -203,12 +204,14 @@
                         )
                         pl.semaphore_signal(barrier, inc=1, device_id=peer, device_id_type=MESH)
                         count += 1
-    pl.semaphore_signal(barrier, inc=1, device_id=y_peer, device_id_type=MESH)
+    for dc in range(2):
+        peer = device(half, low, x, 1 - y, (core + dc) % 2)
+        pl.semaphore_signal(barrier, inc=1, device_id=peer, device_id_type=MESH)
     load(0, w_ref, w_buf)
     load(1, q_ref, q_buf)
     load(2, k_ref, k_buf)
     load(3, t_ref, t_buf)
-    pl.semaphore_wait(barrier, count + 1)
+    pl.semaphore_wait(barrier, count + 2)
 
     pending, far_pending, near_pending = [], [], []
 
@@ -243,7 +246,7 @@
         def _():
             copy.wait_recv()
 
-    def send_inputs(s, picks):
+    def send_inputs(s, picks, cond=None, keep=None):
         for a, b, dc in picks:
             l2, x2, c2 = (low + a) % 2, (x + b) % 2, (core + dc) % 2
             i = a * 4 + b * 2 + dc
@@ -252,14 +255,18 @@
             ]
             dst = feat.at[s, at(me * length, length)]
             args = (src, dst, in_s.at[s, i], in_r.at[s, me], device(core, l2, x2, y, c2))
-            if i:
+            if i and cond is None:
                 send(*args)
+            elif i:
+                send_if(cond, keep, *args)
             else:
-                send_if(far, far_pending, *args)
-
-                @pl.when(near)
-                def _():
-                    pltpu.make_async_copy(src, dst, in_r.at[s, me]).start()
+                if cond is not near:
+                    send_if(far if cond is None else cond, far_pending if cond is None else keep, *args)
+                if cond is None or cond is near:
+
+                    @pl.when(near)
+                    def _():
+                        pltpu.make_async_copy(src, dst, in_r.at[s, me]).start()
 
     def wait_input(s, j):
         slot = feat.at[s, at(j * length, length)]
@@ -296,13 +303,12 @@
             return carry
 
         lax.fori_loop(0, heads, one, 0)
-        first = send_if(
-            far, far_pending, mat.at[0, s], mat.at[1, s], mat_s.at[s, 0], mat_r.at[s, 0], partner
-        )
-        second = send_if(
-            far, far_pending, base.at[0, s], base.at[1, s], mat_s.at[s, 1], mat_r.at[s, 1], partner
-        )
-        return first, second
+
+    def send_products(s, cond, keep):
+        return [
+            send_if(cond, keep, buf.at[0, s], buf.at[1, s], mat_s.at[s, i], mat_r.at[s, i], partner)
+            for i, buf in enumerate((mat, base))
+        ]
 
     chunk = 32
 
@@ -327,127 +333,149 @@
         far, far_pending, wb.at[0, w_mine], wb.at[1, w_mine], w_s.at[0], w_r.at[0], partner
     )
     send_inputs(0, order[4:])
+    for s in range(1, steps):
+        send_inputs(s, order, near, near_pending)
     for i in (1, 2, 3):
         loads[i].wait()
-    mats = [attention_of(0)]
+    attention_of(0)
+    products = [send_products(0, far, far_pending)]
+    for s in range(1, steps):
+        send_inputs(s, order, beside, far_pending)
     wait_if(far, w_cross)
     w_relay = send_if(
         far, far_pending, wb.at[1, w_mine], wb.at[1, w_mine], w_s.at[1], w_r.at[1], y_peer
     )
-    later = {s: list(order) for s in range(1, steps)}
     for s in range(1, steps):
-        send_inputs(s, later[s][:2])
-        later[s] = later[s][2:]
-        mats.append(attention_of(s))
+        attention_of(s)
+        products.append(send_products(s, beside, far_pending))
     wait_if(far, w_relay)
 
     def weights(s, p):
         return wb[sel, :, wide[p]] if s == 0 else w_now[:, wide[p]]
 
+    sides = ((half * quad, near, far, near_pending, far_pending),
+             ((1 - half) * quad, far, near, far_pending, near_pending))
+    slot = at(me_slot(core, low, x) * length, length)
     for s in range(steps):
-        def feed(k):
-            if s + 1 < steps:
-                send_inputs(s + 1, later[s + 1][:k])
-                later[s + 1] = later[s + 1][k:]
-
-        for a, b in quads:
-            wait_input(s, (1 - core) * 4 + ((low + a) % 2) * 2 + (x + b) % 2)
-        pairs = {}
-        for a in (1, 0):
-            start = ((low + a) % 2) * 2 * length
-            span = at(start, 2 * length)
+
+        def scatter(start, taker, giver, keep, keep_giver):
+            for a, b in quads:
+                wait_input(s, start // length + ((low + a) % 2) * 2 + (x + b) % 2)
+            pairs, reds = {}, {}
             for p in range(parts):
-                part = jnp.dot(
-                    feat[s, at(theirs + start, 2 * length)],
-                    weights(s, p),
+                for a in (1, 0):
+                    first = ((low + a) % 2) * 2 * length
+                    span = at(first, 2 * length)
+                    part = jnp.dot(
+                        feat[s, at(start + first, 2 * length)],
+                        weights(s, p),
+                        preferred_element_type=jnp.float32,
+                    )
+                    own_part[span, wide[p]] = part
+
+                    @pl.when(giver)
+                    def _():
+                        pair_out[s, span, wide[p]] = part.astype(jnp.bfloat16)
+
+                    pairs[a, p] = send_if(
+                        giver,
+                        keep_giver,
+                        pair_out.at[s, span, wide[p]],
+                        pair_in.at[s, span, wide[p]],
+                        pair_s.at[s, a, p],
+                        pair_r.at[s, a, p],
+                        core_peer,
+                    )
+            for p in range(parts):
+                for a in (1, 0):
+                    span = at(((low + a) % 2) * 2 * length, 2 * length)
+                    wait_if(taker, pairs[a, p])
+
+                    @pl.when(taker)
+                    def _():
+                        red_out[s, span, wide[p]] = (
+                            own_part[span, wide[p]]
+                            + pair_in[s, span, wide[p]].astype(jnp.float32)
+                        ).astype(jnp.bfloat16)
+
+                    for b in (1, 0):
+                        if a + b:
+                            reds[a, b, p] = send_if(
+                                taker,
+                                keep,
+                                red_out.at[s, at(offset(a, b), length), wide[p]],
+                                red_in.at[s, a * 2 + b, :, wide[p]],
+                                red_s.at[s, a * 2 + b, p],
+                                red_r.at[s, a * 2 + b, p],
+                                mate(a, b),
+                            )
+            return reds
+
+        def reduce(reds, start, taker, giver, keep, keep_giver):
+            gathers, passes = {}, {}
+            for p in range(parts):
+                for a, b in quads[:3]:
+                    wait_if(taker, reds[a, b, p])
+
+                @pl.when(taker)
+                def _():
+                    summed = red_out[s, at(offset(0, 0), length), wide[p]].astype(jnp.float32)
+                    for a, b in quads[:3]:
+                        summed = summed + red_in[s, a * 2 + b, :, wide[p]].astype(jnp.float32)
+                    values = (summed / math.sqrt(D)).astype(jnp.bfloat16)
+                    for i in range(width // HD):
+                        g = p * (width // HD) + i
+                        part = values[:, i * HD : (i + 1) * HD]
+                        vg = jnp.dot(mat[sel, s, g], part, preferred_element_type=jnp.float32)
+                        vg = (vg - base[sel, s, g].astype(jnp.float32)) / tok_rep
+                        vgrad[s, slot, g * HD : (g + 1) * HD] = vg.astype(jnp.bfloat16)
+
+                block = vgrad.at[s, slot, wide[p]]
+                for a, b in quads[:3]:
+                    i = a * 2 + b
+                    gathers[a, b, p] = send_if(
+                        taker, keep, block, block, ag_s.at[s, i, p], ag_r.at[s, i, p], mate(a, b)
+                    )
+                passes[0, 0, p] = send_if(
+                    taker, keep, block, block, fw_s.at[s, 0, p], fw_r.at[s, 0, p], core_peer
+                )
+            return gathers, passes
+
+        def gather(copies, first, start, taker, giver, keep, keep_giver):
+            gathers, passes = copies
+            for p in range(parts):
+                for a, b in quads[2::-1]:
+                    wait_if(taker, gathers[a, b, p])
+                    i = a * 2 + b
+                    block = vgrad.at[s, at(start + offset(a, b), length), wide[p]]
+                    passes[a, b, p] = send_if(
+                        taker, keep, block, block, fw_s.at[s, i, p], fw_r.at[s, i, p], core_peer
+                    )
+            for p in range(parts):
+                for a, b in quads[::-1]:
+                    wait_if(giver, passes[a, b, p])
+                term = lax.dot_general(
+                    feat[s, at(start, quad)],
+                    vgrad[s, at(start, quad), wide[p]],
+                    (((0,), (0,)), ((), ())),
                     preferred_element_type=jnp.float32,
                 )
-                pair_out[s, span, wide[p]] = part.astype(jnp.bfloat16)
-                pairs[a, p] = send(
-                    pair_out.at[s, span, wide[p]],
-                    pair_in.at[s, span, wide[p]],
-                    pair_s.at[s, a, p],
-                    pair_r.at[s, a, p],
-                    core_peer,
-                )
-        for a, b in quads:
-            wait_input(s, core * 4 + ((low + a) % 2) * 2 + (x + b) % 2)
-        reds = {}
-        for p in range(parts):
-            for a in (1, 0):
-                start = ((low + a) % 2) * 2 * length
-                span = at(start, 2 * length)
-                own = jnp.dot(
-                    feat[s, at(mine + start, 2 * length)],
-                    weights(s, p),
-                    preferred_element_type=jnp.float32,
-                )
-                pairs[a, p].wait_recv()
-                own = own + pair_in[s, span, wide[p]].astype(jnp.float32)
-                red_out[s, span, wide[p]] = own.astype(jnp.bfloat16)
-                for b in (1, 0):
-                    if a + b:
-                        reds[a, b, p] = send(
-                            red_out.at[s, at(offset(a, b), length), wide[p]],
-                            red_in.at[s, a * 2 + b, :, wide[p]],
-                            red_s.at[s, a * 2 + b, p],
-                            red_r.at[s, a * 2 + b, p],
-                            mate(a, b),
-                        )
-        feed(2)
-        for copy in mats[s]:
+                if first:
+                    grad[s, :, wide[p]] = term
+                else:
+                    grad[s, :, wide[p]] += term
+
+        near_reds = scatter(*sides[0])
+        near_copies = reduce(near_reds, *sides[0])
+        far_reds = scatter(*sides[1])
+        gather(near_copies, True, *sides[0])
+        for copy in products[s]:
             wait_if(far, copy)
-        gathers, passes = {}, {}
-        slot = at(me_slot(core, low, x) * length, length)
-        for p in range(parts):
-            summed = red_out[s, at(offset(0, 0), length), wide[p]].astype(jnp.float32)
-            for a, b in quads[:3]:
-                reds[a, b, p].wait_recv()
-                summed = summed + red_in[s, a * 2 + b, :, wide[p]].astype(jnp.float32)
-            values = (summed / math.sqrt(D)).astype(jnp.bfloat16)
-            for i in range(width // HD):
-                g = p * (width // HD) + i
-                part = values[:, i * HD : (i + 1) * HD]
-                vg = jnp.dot(mat[sel, s, g], part, preferred_element_type=jnp.float32)
-                vg = (vg - base[sel, s, g].astype(jnp.float32)) / tok_rep
-                vgrad[s, slot, g * HD : (g + 1) * HD] = vg.astype(jnp.bfloat16)
-            block = vgrad.at[s, slot, wide[p]]
-            for a, b in quads[:3]:
-                i = a * 2 + b
-                gathers[a, b, p] = send(
-                    block, block, ag_s.at[s, i, p], ag_r.at[s, i, p], mate(a, b)
-                )
-            passes[0, 0, p] = send(
-                block, block, fw_s.at[s, 0, p], fw_r.at[s, 0, p], core_peer
-            )
-        feed(2)
-
-        def add_quad(start, p, first):
-            term = lax.dot_general(
-                feat[s, at(start, quad)],
-                vgrad[s, at(start, quad), wide[p]],
-                (((0,), (0,)), ((), ())),
-                preferred_element_type=jnp.float32,
-            )
-            if first:
-                grad[s, :, wide[p]] = term
-            else:
-                grad[s, :, wide[p]] += term
-
-        for p in range(parts):
-            for a, b in quads[2::-1]:
-                gathers[a, b, p].wait_recv()
-                i = a * 2 + b
-                block = vgrad.at[s, at(mine + offset(a, b), length), wide[p]]
-                passes[a, b, p] = send(
-                    block, block, fw_s.at[s, i, p], fw_r.at[s, i, p], core_peer
-                )
-            add_quad(mine, p, True)
-        feed(8)
-        for p in range(parts):
-            for a, b in quads:
-                passes[a, b, p].wait_recv()
-            add_quad(theirs, p, False)
+        far_copies = reduce(far_reds, *sides[1])
+        for later in range(s + 1, min(s + 2, steps)):
+            send_inputs(later, order, outer, [])
+            send_products(later, outer, [])
+        gather(far_copies, False, *sides[1])
 
         def adam(r, keep):
             c = at(r, chunk)
@@ -473,10 +501,9 @@
     def moved(c, update):
         return inner_rate * (shrink * first_update[c, :] + update)
 
-    pieces = 2
+    pieces = 4
     size = mid // pieces
-    sub = size // 2
-    firsts, seconds, thirds, fourths, fifths = [], [], [], [], []
+    crosses, sums, overs, shared, third, fourth = [], [], [], [], [], []
     for p in range(pieces):
 
         def out_piece(r):
@@ -487,21 +514,20 @@
 
         over(0, size, out_piece)
         piece = at(p * size, size)
-        firsts.append(
+        crosses.append(
             send(sy_out.at[piece], sy_in.at[piece], fin_s.at[0, p], fin_r.at[0, p], y_peer)
         )
-    for p in range(pieces):
-
-        def own_piece(r):
-            def put(c, update):
-                s_own[at(p * size + r, chunk), :] = moved(c, update)
-
-            adam(y * mid + p * size + r, put)
-
-        over(0, size, own_piece)
+
+    def own_rows(r):
+        def put(c, update):
+            s_own[at(r, chunk), :] = moved(c, update)
+
+        adam(y * mid + r, put)
+
+    over(0, mid, own_rows)
     for p in range(pieces):
         piece = at(p * size, size)
-        firsts[p].wait_recv()
+        crosses[p].wait_recv()
 
         def join(r):
             c = at(p * size + r, chunk)
@@ -510,7 +536,18 @@
             )
 
         over(0, size, join)
-        seconds.append(
+        overs.append(
+            send_if(
+                far,
+                far_pending,
+                halves.at[2, piece],
+                halves.at[1, piece],
+                fin_s.at[2, p],
+                fin_r.at[2, p],
+                partner,
+            )
+        )
+        sums.append(
             send_if(
                 near,
                 near_pending,
@@ -521,65 +558,46 @@
                 core_peer,
             )
         )
-        thirds.append(
-            send_if(
-                far,
-                far_pending,
-                halves.at[2, piece],
-                halves.at[1, piece],
-                fin_s.at[2, p],
-                fin_r.at[2, p],
-                partner,
-            )
-        )
-    replicas = 4
+    y_cross = device(half, low, x, 1 - y, 1 - core)
+
+    def copy_out(start, src):
+        def one(r):
+            mean_ref[at(start + r, chunk), :] = src(r)
+
+        over(0, size, one)
+
     for p in range(pieces):
         piece = at(p * size, size)
-        wait_if(far, thirds[p])
-        fourths.append(
-            send_if(
-                far,
-                far_pending,
-                halves.at[1, piece],
-                halves.at[1, piece],
-                fin_s.at[3, p],
-                fin_r.at[3, p],
-                core_peer,
-            )
-        )
-        wait_if(far, seconds[p])
-        wait_if(near, fourths[p])
-
-        def total(r):
-            c = at(p * size + r, chunk)
-            both = (
-                halves[0, c, :].astype(jnp.float32) + halves[1, c, :].astype(jnp.float32)
-            ).astype(jnp.bfloat16)
-            tot_mine[c, :] = both
-            mean_ref[at(y * mid + p * size + r, chunk), :] = both.astype(jnp.float32) / replicas
-
-        over(0, size, total)
-        bit = at(p * size + core * sub, sub)
-        fifths.append(
-            send(tot_mine.at[bit], tot_other.at[bit], fin_s.at[4, p], fin_r.at[4, p], y_peer)
-        )
-    sixths = []
+        wait_if(far, sums[p])
+        wait_if(far, overs[p])
+
+        @pl.when(far)
+        def _():
+            def one(r):
+                c = at(p * size + r, chunk)
+                tot_mine[c, :] = (
+                    halves[0, c, :].astype(jnp.float32) + halves[1, c, :].astype(jnp.float32)
+                ).astype(jnp.bfloat16)
+
+            over(0, size, one)
+
+        mine_p, other_p = tot_mine.at[piece], tot_other.at[piece]
+        third.append(
+            send_if(far, far_pending, mine_p, other_p, fin_s.at[3, p], fin_r.at[3, p], y_peer)
+        )
+        fourth.append(
+            send_if(far, far_pending, mine_p, other_p, fin_s.at[4, p], fin_r.at[4, p], y_cross)
+        )
+        shared.append(
+            send_if(far, far_pending, mine_p, mine_p, fin_s.at[5, p], fin_r.at[5, p], core_peer)
+        )
     for p in range(pieces):
-        bit = at(p * size + core * sub, sub)
-        fifths[p].wait_recv()
-        sixths.append(
-            send(tot_other.at[bit], tot_other.at[bit], fin_s.at[5, p], fin_r.at[5, p], core_peer)
-        )
+        wait_if(near, shared[p])
+        copy_out(y * mid + p * size, lambda r: tot_mine[at(p * size + r, chunk), :])
     for p in range(pieces):
-        sixths[p].wait_recv()
-
-        def finish(r):
-            c = at(p * size + r, chunk)
-            mean_ref[at((1 - y) * mid + p * size + r, chunk), :] = (
-                tot_other[c, :].astype(jnp.float32) / replicas
-            )
-
-        over(0, size, finish)
+        wait_if(far, third[p])
+        wait_if(near, fourth[p])
+        copy_out((1 - y) * mid + p * size, lambda r: tot_other[at(p * size + r, chunk), :])
     for copy in pending:
         copy.wait_send()
 
@@ -608,8 +626,8 @@
     heads = columns // HD
     bf, f32 = jnp.bfloat16, jnp.float32
     dma = pltpu.SemaphoreType.DMA
-    out = jax.ShapeDtypeStruct((rows, columns), f32)
-    mean_update = pl.pallas_call(
+    out = jax.ShapeDtypeStruct((rows, columns), bf)
+    total_update = pl.pallas_call(
         round_kernel,
         out_shape=out,
         in_specs=[pl.BlockSpec(memory_space=pl.ANY)] * 5,
@@ -622,6 +640,7 @@
             pltpu.VMEM((rows, columns), f32),
             pltpu.VMEM((2, rows, columns), bf),
             pltpu.VMEM((rows, columns), bf),
+            pltpu.VMEM((4 * length, columns), f32),
             pltpu.VMEM((2, steps, heads, length, length), bf),
             pltpu.VMEM((2, steps, heads, length, HD), bf),
             pltpu.VMEM((steps, 4 * length, columns), bf),
@@ -651,14 +670,14 @@
             dma((steps, 4, 2)),
             dma((steps, 4, 2)),
             dma((steps, 4, 2)),
-            dma((6, 2)),
-            dma((6, 2)),
+            dma((6, 4)),
+            dma((6, 4)),
             dma((4,)),
         ],
         compiler_params=pltpu.CompilerParams(collective_id=0, has_side_effects=True),
     )(layer_input, queries, keys, targets, value_weight)
     kept = (1.0 - inner_rate * decay_rate) ** steps
-    mean_delta = (1.0 - kept) * value_weight + mean_update
+    mean_delta = (1.0 - kept) * value_weight + total_update.astype(f32) / replicas
     new_momentum = outer_mu * outer_momentum + mean_delta
     new_weight = value_weight - outer_rate * (mean_delta + outer_mu * new_momentum)
     return (new_weight, new_momentum)

time: 117 us -> 114 us (0.974)
  Pallas kernels: 113 us -> 111 us
    pallas_call x1, Pallas kernels: 113 us -> 111 us  [shards(): pl.pallas_call(round_kernel, out_shape=out, in_specs=[pl.BlockSpec(memory...]
where the time goes in v2:
time: 114 us
  Pallas kernels  111 us (97%)
  other arithmetic  2.73 us (2%)
    pallas_call x1, Pallas kernels, shards(): pl.pallas_call(round_kernel, out_shape=out, in_specs=[pl.BlockSpec(memory...  111 us
    sub x1, other arithmetic, shards(): value_weight - outer_rate * (mean_delta + outer_mu * new_momentum)  2.73 us

profile of v2, /device:TPU:0, one launch (start us, length us, event | category | flops | bytes accessed | tf_op | source)
XLA Modules:
  0.0 114.2 jit_solution(5069251033663983519)
XLA Ops:
  0.6 0.0 copy-start
  0.6 0.0 copy-start.1
  0.7 110.8 %shard_map.77 = bf16[512,512]{1,0:T(8,128)(2,1)} custom-call(bf16[2,128,4096]{2,1,0:T(8,128)(2,1)} %x_ref.1, bf16[2,128,4096]{2,1,0:T(8,128)(2,1)} %q_ref.1, bf16[2,128,512]{2,1,0:T(8,128)(2,1)} %k_ref.1, bf16[2,128,4096]{2,1,0:T(8,128)(2,1)} %t_ref.1, f32[512,512]{1,0:T(8,128)} %w_ref.1), custom_call_target="tpu_custom_call" | custom-call | tf_op jit(solution)/shard_map/pallas_call | solution.py:630
  111.5 0.0 copy-done
  111.5 0.0 copy-done.1
  111.5 2.7 %multiply_subtract_fusion = (f32[512,512]{1,0:T(8,128)}, f32[512,512]{1,0:T(8,128)}) fusion(f32[512,512]{1,0:T(8,128)S(1)} %copy-done, bf16[512,512]{1,0:T(8,128)(2,1)} %shard_map.77, f32[512,512]{1,0:T(8,128)S(1)} %copy-done.1), kind=kLoop, calls=%fused_computation | loop fusion | flops 2621440 | bytes 4718592 | tf_op jit(solution)/shard_map/sub | solution.py:682
Async XLA Ops:
  0.6 110.8 %copy-start = (f32[512,512]{1,0:T(8,128)S(1)}, f32[512,512]{1,0:T(8,128)}, u32[]{:S(2)}) copy-start(f32[512,512]{1,0:T(8,128)} %w_ref.1) | copy-start | bytes 3145732
  0.6 110.8 %copy-start.1 = (f32[512,512]{1,0:T(8,128)S(1)}, f32[512,512]{1,0:T(8,128)}, u32[]{:S(2)}) copy-start(f32[512,512]{1,0:T(8,128)} %param.11) | copy-start | bytes 3145732

commit v3 on v2

--- a/solution.py
+++ b/solution.py
@@ -347,7 +347,6 @@
     )
     for s in range(1, steps):
         attention_of(s)
-        products.append(send_products(s, beside, far_pending))
     wait_if(far, w_relay)
 
     def weights(s, p):
@@ -441,53 +440,61 @@
                 )
             return gathers, passes
 
-        def gather(copies, first, start, taker, giver, keep, keep_giver):
+        def forward(copies, p, start, taker, giver, keep, keep_giver):
             gathers, passes = copies
-            for p in range(parts):
-                for a, b in quads[2::-1]:
-                    wait_if(taker, gathers[a, b, p])
-                    i = a * 2 + b
-                    block = vgrad.at[s, at(start + offset(a, b), length), wide[p]]
-                    passes[a, b, p] = send_if(
-                        taker, keep, block, block, fw_s.at[s, i, p], fw_r.at[s, i, p], core_peer
-                    )
-            for p in range(parts):
-                for a, b in quads[::-1]:
-                    wait_if(giver, passes[a, b, p])
-                term = lax.dot_general(
-                    feat[s, at(start, quad)],
-                    vgrad[s, at(start, quad), wide[p]],
-                    (((0,), (0,)), ((), ())),
-                    preferred_element_type=jnp.float32,
+            for a, b in quads[2::-1]:
+                wait_if(taker, gathers[a, b, p])
+                i = a * 2 + b
+                block = vgrad.at[s, at(start + offset(a, b), length), wide[p]]
+                passes[a, b, p] = send_if(
+                    taker, keep, block, block, fw_s.at[s, i, p], fw_r.at[s, i, p], core_peer
                 )
-                if first:
-                    grad[s, :, wide[p]] = term
-                else:
-                    grad[s, :, wide[p]] += term
+
+        def add_quad(copies, first, p, start, taker, giver, keep, keep_giver):
+            for a, b in quads[::-1]:
+                wait_if(giver, copies[1][a, b, p])
+            term = lax.dot_general(
+                feat[s, at(start, quad)],
+                vgrad[s, at(start, quad), wide[p]],
+                (((0,), (0,)), ((), ())),
+                preferred_element_type=jnp.float32,
+            )
+            if first:
+                grad[s, :, wide[p]] = term
+            else:
+                grad[s, :, wide[p]] += term
 
         near_reds = scatter(*sides[0])
+        if s:
+            products.append(send_products(s, far, far_pending))
         near_copies = reduce(near_reds, *sides[0])
         far_reds = scatter(*sides[1])
-        gather(near_copies, True, *sides[0])
+        if s + 1 < steps:
+            send_inputs(s + 1, order[:2], outer, [])
+        for p in range(parts):
+            forward(near_copies, p, *sides[0])
+        for p in range(parts):
+            add_quad(near_copies, True, p, *sides[0])
         for copy in products[s]:
             wait_if(far, copy)
         far_copies = reduce(far_reds, *sides[1])
-        for later in range(s + 1, min(s + 2, steps)):
-            send_inputs(later, order, outer, [])
-            send_products(later, outer, [])
-        gather(far_copies, False, *sides[1])
-
-        def adam(r, keep):
+        if s + 1 < steps:
+            send_inputs(s + 1, order[2:], outer, [])
+            for p in range(parts):
+                forward(far_copies, p, *sides[1])
+            for p in range(parts):
+                add_quad(far_copies, False, p, *sides[1])
+
+        def adam(r, cols, keep):
             c = at(r, chunk)
             one, two = 0.0, 0.0
             for i in range(s + 1):
-                gradient = grad[i, c, :] / math.sqrt(D)
+                gradient = grad[i, c, cols] / math.sqrt(D)
                 one = beta_one * one + (1.0 - beta_one) * gradient
                 two = beta_two * two + (1.0 - beta_two) * gradient * gradient
             fixed_one = one / (1.0 - beta_one ** (s + 1))
             fixed_two = two / (1.0 - beta_two ** (s + 1))
-            update = fixed_one / (jnp.sqrt(fixed_two) + adam_floor)
-            keep(c, update)
+            keep(c, fixed_one / (jnp.sqrt(fixed_two) + adam_floor))
 
         if s + 1 < steps:
 
@@ -496,108 +503,119 @@
                 first_update[c, :] = update
                 w_now[c, :] = (before * shrink - inner_rate * update).astype(jnp.bfloat16)
 
-            over(0, rows, lambda r: adam(r, keep))
-
-    def moved(c, update):
-        return inner_rate * (shrink * first_update[c, :] + update)
-
-    pieces = 4
+            over(0, rows, lambda r: adam(r, slice(None), keep))
+
+    pieces = 2
     size = mid // pieces
-    crosses, sums, overs, shared, third, fourth = [], [], [], [], [], []
-    for p in range(pieces):
-
-        def out_piece(r):
+    crosses, sums, overs, shared, third, fourth = {}, {}, {}, {}, {}, {}
+    cells = [(p, i) for p in range(parts) for i in range(pieces)]
+
+    def moved(c, cols, update):
+        return inner_rate * (shrink * first_update[c, cols] + update)
+
+    def cell(ref, p, i):
+        return ref.at[at(i * size, size), wide[p]]
+
+    for p in range(parts):
+        forward(far_copies, p, *sides[1])
+        add_quad(far_copies, False, p, *sides[1])
+        for i in range(pieces):
+
+            def out_rows(r):
+                def put(c, update):
+                    sy_out[at(i * size + r, chunk), wide[p]] = moved(c, wide[p], update).astype(
+                        jnp.bfloat16
+                    )
+
+                adam((1 - y) * mid + i * size + r, wide[p], put)
+
+            over(0, size, out_rows)
+            k = p * pieces + i
+            crosses[p, i] = send(
+                cell(sy_out, p, i), cell(sy_in, p, i), fin_s.at[0, k], fin_r.at[0, k], y_peer
+            )
+    for p in range(parts):
+
+        def own_rows(r):
             def put(c, update):
-                sy_out[at(p * size + r, chunk), :] = moved(c, update).astype(jnp.bfloat16)
-
-            adam((1 - y) * mid + p * size + r, put)
-
-        over(0, size, out_piece)
-        piece = at(p * size, size)
-        crosses.append(
-            send(sy_out.at[piece], sy_in.at[piece], fin_s.at[0, p], fin_r.at[0, p], y_peer)
-        )
-
-    def own_rows(r):
-        def put(c, update):
-            s_own[at(r, chunk), :] = moved(c, update)
-
-        adam(y * mid + r, put)
-
-    over(0, mid, own_rows)
-    for p in range(pieces):
-        piece = at(p * size, size)
-        crosses[p].wait_recv()
+                s_own[at(r, chunk), wide[p]] = moved(c, wide[p], update)
+
+            adam(y * mid + r, wide[p], put)
+
+        over(0, mid, own_rows)
+    for p, i in cells:
+        k = p * pieces + i
+        crosses[p, i].wait_recv()
 
         def join(r):
-            c = at(p * size + r, chunk)
-            halves[2 * sel, c, :] = (s_own[c, :] + sy_in[c, :].astype(jnp.float32)).astype(
-                jnp.bfloat16
-            )
+            c = at(i * size + r, chunk)
+            halves[2 * sel, c, wide[p]] = (
+                s_own[c, wide[p]] + sy_in[c, wide[p]].astype(jnp.float32)
+            ).astype(jnp.bfloat16)
 
         over(0, size, join)
-        overs.append(
-            send_if(
-                far,
-                far_pending,
-                halves.at[2, piece],
-                halves.at[1, piece],
-                fin_s.at[2, p],
-                fin_r.at[2, p],
-                partner,
-            )
-        )
-        sums.append(
-            send_if(
-                near,
-                near_pending,
-                halves.at[0, piece],
-                halves.at[0, piece],
-                fin_s.at[1, p],
-                fin_r.at[1, p],
-                core_peer,
-            )
+        overs[p, i] = send_if(
+            far,
+            far_pending,
+            cell(halves.at[2], p, i),
+            cell(halves.at[1], p, i),
+            fin_s.at[2, k],
+            fin_r.at[2, k],
+            partner,
+        )
+        sums[p, i] = send_if(
+            near,
+            near_pending,
+            cell(halves.at[0], p, i),
+            cell(halves.at[0], p, i),
+            fin_s.at[1, k],
+            fin_r.at[1, k],
+            core_peer,
         )
     y_cross = device(half, low, x, 1 - y, 1 - core)
 
-    def copy_out(start, src):
-        def one(r):
-            mean_ref[at(start + r, chunk), :] = src(r)
-
-        over(0, size, one)
-
-    for p in range(pieces):
-        piece = at(p * size, size)
-        wait_if(far, sums[p])
-        wait_if(far, overs[p])
+    for p, i in cells:
+        k = p * pieces + i
+        wait_if(far, sums[p, i])
+        wait_if(far, overs[p, i])
 
         @pl.when(far)
         def _():
             def one(r):
-                c = at(p * size + r, chunk)
-                tot_mine[c, :] = (
-                    halves[0, c, :].astype(jnp.float32) + halves[1, c, :].astype(jnp.float32)
+                c = at(i * size + r, chunk)
+                tot_mine[c, wide[p]] = (
+                    halves[0, c, wide[p]].astype(jnp.float32)
+                    + halves[1, c, wide[p]].astype(jnp.float32)
                 ).astype(jnp.bfloat16)
 
             over(0, size, one)
 
-        mine_p, other_p = tot_mine.at[piece], tot_other.at[piece]
-        third.append(
-            send_if(far, far_pending, mine_p, other_p, fin_s.at[3, p], fin_r.at[3, p], y_peer)
-        )
-        fourth.append(
-            send_if(far, far_pending, mine_p, other_p, fin_s.at[4, p], fin_r.at[4, p], y_cross)
-        )
-        shared.append(
-            send_if(far, far_pending, mine_p, mine_p, fin_s.at[5, p], fin_r.at[5, p], core_peer)
-        )
-    for p in range(pieces):
-        wait_if(near, shared[p])
-        copy_out(y * mid + p * size, lambda r: tot_mine[at(p * size + r, chunk), :])
-    for p in range(pieces):
-        wait_if(far, third[p])
-        wait_if(near, fourth[p])
-        copy_out((1 - y) * mid + p * size, lambda r: tot_other[at(p * size + r, chunk), :])
+        mine_p, other_p = cell(tot_mine, p, i), cell(tot_other, p, i)
+        third[p, i] = send_if(
+            far, far_pending, mine_p, other_p, fin_s.at[3, k], fin_r.at[3, k], y_peer
+        )
+        fourth[p, i] = send_if(
+            far, far_pending, mine_p, other_p, fin_s.at[4, k], fin_r.at[4, k], y_cross
+        )
+        shared[p, i] = send_if(
+            far, far_pending, mine_p, mine_p, fin_s.at[5, k], fin_r.at[5, k], core_peer
+        )
+
+    def copy_out(start, p, i, src):
+        def one(r):
+            mean_ref[at(start + i * size + r, chunk), wide[p]] = src[
+                at(i * size + r, chunk), wide[p]
+            ]
+
+        over(0, size, one)
+
+    for p, i in cells:
+        wait_if(near, shared[p, i])
+        copy_out(y * mid, p, i, tot_mine)
+    for p, i in cells:
+        wait_if(far, third[p, i])
+        wait_if(near, fourth[p, i])
+        copy_out((1 - y) * mid, p, i, tot_other)
     for copy in pending:
         copy.wait_send()
 

time: 114 us -> 108 us (0.947)
  Pallas kernels: 111 us -> 104 us
    pallas_call x1, Pallas kernels: 111 us -> 104 us  [shards(): pl.pallas_call(round_kernel, out_shape=out, in_specs=[pl.BlockSpec(memory...]
where the time goes in v3:
time: 108 us
  Pallas kernels  104 us (96%)
  other arithmetic  2.73 us (3%)
    pallas_call x1, Pallas kernels, shards(): pl.pallas_call(round_kernel, out_shape=out, in_specs=[pl.BlockSpec(memory...  104 us
    sub x1, other arithmetic, shards(): value_weight - outer_rate * (mean_delta + outer_mu * new_momentum)  2.73 us

profile of v3, /device:TPU:0, one launch (start us, length us, event | category | flops | bytes accessed | tf_op | source)
XLA Modules:
  0.0 107.9 jit_solution(5581852727770862708)
XLA Ops:
  0.6 0.0 copy-start
  0.6 0.0 copy-start.1
  0.7 104.5 %shard_map.77 = bf16[512,512]{1,0:T(8,128)(2,1)} custom-call(bf16[2,128,4096]{2,1,0:T(8,128)(2,1)} %x_ref.1, bf16[2,128,4096]{2,1,0:T(8,128)(2,1)} %q_ref.1, bf16[2,128,512]{2,1,0:T(8,128)(2,1)} %k_ref.1, bf16[2,128,4096]{2,1,0:T(8,128)(2,1)} %t_ref.1, f32[512,512]{1,0:T(8,128)} %w_ref.1), custom_call_target="tpu_custom_call" | custom-call | tf_op jit(solution)/shard_map/pallas_call | solution.py:648
  105.2 0.0 copy-done
  105.2 0.0 copy-done.1
  105.2 2.7 %multiply_subtract_fusion = (f32[512,512]{1,0:T(8,128)}, f32[512,512]{1,0:T(8,128)}) fusion(f32[512,512]{1,0:T(8,128)S(1)} %copy-done, bf16[512,512]{1,0:T(8,128)(2,1)} %shard_map.77, f32[512,512]{1,0:T(8,128)S(1)} %copy-done.1), kind=kLoop, calls=%fused_computation | loop fusion | flops 2621440 | bytes 4718592 | tf_op jit(solution)/shard_map/sub | solution.py:700
Async XLA Ops:
  0.6 104.5 %copy-start = (f32[512,512]{1,0:T(8,128)S(1)}, f32[512,512]{1,0:T(8,128)}, u32[]{:S(2)}) copy-start(f32[512,512]{1,0:T(8,128)} %w_ref.1) | copy-start | bytes 3145732
  0.6 104.5 %copy-start.1 = (f32[512,512]{1,0:T(8,128)S(1)}, f32[512,512]{1,0:T(8,128)}, u32[]{:S(2)}) copy-start(f32[512,512]{1,0:T(8,128)} %param.11) | copy-start | bytes 3145732

commit v4 on v3

--- a/solution.py
+++ b/solution.py
@@ -320,7 +320,6 @@
         lax.fori_loop(0, size // chunk, step, 0)
 
     order = [(a, b, dc) for a, b in quads for dc in (1, 0)]
-    send_inputs(0, order[:4])
     loads[0].wait()
 
     def cast_weights(r):
@@ -332,21 +331,20 @@
     w_cross = send_if(
         far, far_pending, wb.at[0, w_mine], wb.at[1, w_mine], w_s.at[0], w_r.at[0], partner
     )
-    send_inputs(0, order[4:])
+    send_inputs(0, order)
     for s in range(1, steps):
-        send_inputs(s, order, near, near_pending)
+        pass
     for i in (1, 2, 3):
         loads[i].wait()
+    wait_if(far, w_cross)
+    w_relay = send_if(
+        far, far_pending, wb.at[1, w_mine], wb.at[1, w_mine], w_s.at[1], w_r.at[1], y_peer
+    )
     attention_of(0)
     products = [send_products(0, far, far_pending)]
     for s in range(1, steps):
         send_inputs(s, order, beside, far_pending)
-    wait_if(far, w_cross)
-    w_relay = send_if(
-        far, far_pending, wb.at[1, w_mine], wb.at[1, w_mine], w_s.at[1], w_r.at[1], y_peer
-    )
-    for s in range(1, steps):
-        attention_of(s)
+        send_inputs(s, order, near, near_pending)
     wait_if(far, w_relay)
 
     def weights(s, p):
@@ -468,9 +466,11 @@
         if s:
             products.append(send_products(s, far, far_pending))
         near_copies = reduce(near_reds, *sides[0])
+        if s + 1 < steps:
+            attention_of(s + 1)
         far_reds = scatter(*sides[1])
         if s + 1 < steps:
-            send_inputs(s + 1, order[:2], outer, [])
+            send_inputs(s + 1, order[:4], outer, [])
         for p in range(parts):
             forward(near_copies, p, *sides[0])
         for p in range(parts):
@@ -479,7 +479,7 @@
             wait_if(far, copy)
         far_copies = reduce(far_reds, *sides[1])
         if s + 1 < steps:
-            send_inputs(s + 1, order[2:], outer, [])
+            send_inputs(s + 1, order[4:], outer, [])
             for p in range(parts):
                 forward(far_copies, p, *sides[1])
             for p in range(parts):

time: 108 us -> 100 us (0.926)
  Pallas kernels: 104 us -> 96.9 us
    pallas_call x1, Pallas kernels: 104 us -> 96.9 us  [shards(): pl.pallas_call(round_kernel, out_shape=out, in_specs=[pl.BlockSpec(memory...]
where the time goes in v4:
time: 100 us
  Pallas kernels  96.9 us (97%)
  other arithmetic  2.73 us (3%)
    pallas_call x1, Pallas kernels, shards(): pl.pallas_call(round_kernel, out_shape=out, in_specs=[pl.BlockSpec(memory...  96.9 us
    sub x1, other arithmetic, shards(): value_weight - outer_rate * (mean_delta + outer_mu * new_momentum)  2.73 us

profile of v4, /device:TPU:0, one launch (start us, length us, event | category | flops | bytes accessed | tf_op | source)
XLA Modules:
  0.0 100.3 jit_solution(14349166409437117994)
XLA Ops:
  0.6 0.0 copy-start
  0.6 0.0 copy-start.1
  0.7 96.9 %shard_map.77 = bf16[512,512]{1,0:T(8,128)(2,1)} custom-call(bf16[2,128,4096]{2,1,0:T(8,128)(2,1)} %x_ref.1, bf16[2,128,4096]{2,1,0:T(8,128)(2,1)} %q_ref.1, bf16[2,128,512]{2,1,0:T(8,128)(2,1)} %k_ref.1, bf16[2,128,4096]{2,1,0:T(8,128)(2,1)} %t_ref.1, f32[512,512]{1,0:T(8,128)} %w_ref.1), custom_call_target="tpu_custom_call" | custom-call | tf_op jit(solution)/shard_map/pallas_call | solution.py:648
  97.5 0.0 copy-done
  97.5 0.0 copy-done.1
  97.5 2.7 %multiply_subtract_fusion = (f32[512,512]{1,0:T(8,128)}, f32[512,512]{1,0:T(8,128)}) fusion(f32[512,512]{1,0:T(8,128)S(1)} %copy-done, bf16[512,512]{1,0:T(8,128)(2,1)} %shard_map.77, f32[512,512]{1,0:T(8,128)S(1)} %copy-done.1), kind=kLoop, calls=%fused_computation | loop fusion | flops 2621440 | bytes 4718592 | tf_op jit(solution)/shard_map/sub | solution.py:700
Async XLA Ops:
  0.6 96.9 %copy-start = (f32[512,512]{1,0:T(8,128)S(1)}, f32[512,512]{1,0:T(8,128)}, u32[]{:S(2)}) copy-start(f32[512,512]{1,0:T(8,128)} %w_ref.1) | copy-start | bytes 3145732
  0.6 96.9 %copy-start.1 = (f32[512,512]{1,0:T(8,128)S(1)}, f32[512,512]{1,0:T(8,128)}, u32[]{:S(2)}) copy-start(f32[512,512]{1,0:T(8,128)} %param.11) | copy-start | bytes 3145732

commit v5 on v4

--- a/solution.py
+++ b/solution.py
@@ -310,7 +310,7 @@
             for i, buf in enumerate((mat, base))
         ]
 
-    chunk = 32
+    chunk = 64
 
     def over(start, size, body):
         def step(i, carry):

time: 100 us -> 100 us (level)
  no operation moved by 1% of the time
where the time goes in v5:
time: 100 us
  Pallas kernels  96.6 us (97%)
  other arithmetic  2.73 us (3%)
    pallas_call x1, Pallas kernels, shards(): pl.pallas_call(round_kernel, out_shape=out, in_specs=[pl.BlockSpec(memory...  96.6 us
    sub x1, other arithmetic, shards(): value_weight - outer_rate * (mean_delta + outer_mu * new_momentum)  2.73 us

profile of v5, /device:TPU:0, one launch (start us, length us, event | category | flops | bytes accessed | tf_op | source)
XLA Modules:
  0.0 100.0 jit_solution(12874272205878412677)
XLA Ops:
  0.6 0.0 copy-start
  0.6 0.0 copy-start.1
  0.7 96.6 %shard_map.77 = bf16[512,512]{1,0:T(8,128)(2,1)} custom-call(bf16[2,128,4096]{2,1,0:T(8,128)(2,1)} %x_ref.1, bf16[2,128,4096]{2,1,0:T(8,128)(2,1)} %q_ref.1, bf16[2,128,512]{2,1,0:T(8,128)(2,1)} %k_ref.1, bf16[2,128,4096]{2,1,0:T(8,128)(2,1)} %t_ref.1, f32[512,512]{1,0:T(8,128)} %w_ref.1), custom_call_target="tpu_custom_call" | custom-call | tf_op jit(solution)/shard_map/pallas_call | solution.py:648
  97.2 0.0 copy-done
  97.2 0.0 copy-done.1
  97.3 2.7 %multiply_subtract_fusion = (f32[512,512]{1,0:T(8,128)}, f32[512,512]{1,0:T(8,128)}) fusion(f32[512,512]{1,0:T(8,128)S(1)} %copy-done, bf16[512,512]{1,0:T(8,128)(2,1)} %shard_map.77, f32[512,512]{1,0:T(8,128)S(1)} %copy-done.1), kind=kLoop, calls=%fused_computation | loop fusion | flops 2621440 | bytes 4718592 | tf_op jit(solution)/shard_map/sub | solution.py:700
Async XLA Ops:
  0.6 96.6 %copy-start = (f32[512,512]{1,0:T(8,128)S(1)}, f32[512,512]{1,0:T(8,128)}, u32[]{:S(2)}) copy-start(f32[512,512]{1,0:T(8,128)} %w_ref.1) | copy-start | bytes 3145732
  0.6 96.6 %copy-start.1 = (f32[512,512]{1,0:T(8,128)S(1)}, f32[512,512]{1,0:T(8,128)}, u32[]{:S(2)}) copy-start(f32[512,512]{1,0:T(8,128)} %param.11) | copy-start | bytes 3145732
